TPU v7x, 32 devices: a whole 2x2x4 slice. The times are simulated.
32 devices in a mesh: lat: 4 (over x, core), lon: 8 (over z, y).
Axes of the slice: x: 2, y: 2, z: 4, core: 2. Of those that a mesh axis runs over, the one named last changes fastest.
Arguments:
- prediction_fields: float32 [4, 69, 360, 512], P(None, None, 'lon', 'lat'), may hold values from -16 to 16
- verifying_state: float32 [69, 360, 512], P(None, 'lon', 'lat'), may hold values from -16 to 16
- normal_state: float32 [69, 360, 512], P(None, 'lon', 'lat'), may hold values from -16 to 16
- evaluated_point_flag: int32 [360, 512], P('lon', 'lat'), may hold values 0 or 1
- parallels_each_strip: int32 [4], replicated, may hold values from 1 to 128, 361 in all
Outputs:
- parallel_quadratic_error: float32 [4, 69, 512], P(None, None, 'lat')
- parallel_systematic_error: float32 [4, 69, 512], P(None, None, 'lat')
- parallel_pattern_skill: float32 [4, 69, 512], P(None, None, 'lat')
- rmse: float32 [4, 69], replicated
- systematic_error: float32 [4, 69], replicated
- pattern_skill: float32 [4, 69], replicated
Inputs may be any that keep to these rules, and one draw needn't show every extreme that they name: `parallels_each_strip`: they sum to 361, and some band holds exactly 128 rows.
All inputs are finite; a program needn't handle non-finite values.
Results may differ from a plain program's by a relative error of at most 0.00002.
Values sent between devices are 32-bit elements.
A program may use at most 64 MiB of HBM per device.

v0:
```python
import jax
import jax.numpy as jnp
from jax import lax
from jax.sharding import PartitionSpec as P

MEAN_ROWS = 90
minimum_divisor = 0.1


def stacked_metrics(totals, horizon_tally, quantity_tally, grid_point_tally):
    block_rows = horizon_tally * quantity_tally
    width = totals.shape[1]
    error_power_two = (
        totals[:block_rows].reshape(horizon_tally, quantity_tally, width) / grid_point_tally
    )
    prediction_error = (
        totals[block_rows : 2 * block_rows].reshape(horizon_tally, quantity_tally, width)
        / grid_point_tally
    )
    paired_anomaly_term = (
        totals[2 * block_rows : 3 * block_rows].reshape(horizon_tally, quantity_tally, width)
        / grid_point_tally
    )
    predicted_spread_sum = (
        totals[3 * block_rows : 4 * block_rows].reshape(horizon_tally, quantity_tally, width)
        / grid_point_tally
    )
    observed_dispersion = (
        totals[4 * block_rows :].reshape(1, quantity_tally, width) / grid_point_tally
    )
    divisor_term = jnp.sqrt(
        jnp.maximum(predicted_spread_sum, minimum_divisor)
        * jnp.maximum(observed_dispersion, minimum_divisor)
    )
    return (error_power_two, prediction_error, paired_anomaly_term / divisor_term)


def local(
    prediction_fields, verifying_state, normal_state, evaluated_point_flag, parallels_each_strip
):
    horizon_tally, quantity_tally, zonal_circle_size, parallel_index = prediction_fields.shape
    lat_bands = lax.axis_size("lat")
    lon_spokes = lax.axis_size("lon")
    lat_total = MEAN_ROWS * lat_bands + 1
    lon_total = zonal_circle_size * lon_spokes
    band_index = lax.axis_index("lat")
    band_ids = jnp.arange(lat_bands, dtype=jnp.int32)
    first_row = jnp.sum(jnp.where(band_ids < band_index, parallels_each_strip, 0))
    band_filled = jnp.sum(jnp.where(band_ids == band_index, parallels_each_strip, 0))
    slot_ids = jnp.arange(parallel_index, dtype=jnp.int32)
    inside_band = slot_ids < band_filled
    angles = jnp.pi * jnp.arange(lat_total, dtype=jnp.float32) / (lat_total - 1)
    normalizer = jnp.sum(jnp.sin(angles))
    row_angle = jnp.pi * (first_row + slot_ids).astype(jnp.float32) / (lat_total - 1)
    area_factors = jnp.where(inside_band, jnp.sin(row_angle) * lat_total / normalizer, 0.0)
    retain_filter = (
        evaluated_point_flag.astype(jnp.float32) * inside_band.astype(jnp.float32)[None, :]
    )
    observed_anomaly = verifying_state - normal_state
    predicted_anomaly = prediction_fields - normal_state[None]
    mistake_field = predicted_anomaly - observed_anomaly[None]
    retained_entries = retain_filter[None, None]
    block_rows = horizon_tally * quantity_tally
    partial_value = jnp.concatenate(
        [
            jnp.sum(retained_entries * mistake_field * mistake_field, axis=2).reshape(
                block_rows, parallel_index
            ),
            jnp.sum(retained_entries * mistake_field, axis=2).reshape(block_rows, parallel_index),
            jnp.sum(retained_entries * predicted_anomaly * observed_anomaly[None], axis=2).reshape(
                block_rows, parallel_index
            ),
            jnp.sum(retained_entries * predicted_anomaly * predicted_anomaly, axis=2).reshape(
                block_rows, parallel_index
            ),
            jnp.sum(retain_filter[None] * observed_anomaly * observed_anomaly, axis=1),
        ],
        axis=0,
    )
    grand = lax.psum(jnp.sum(partial_value * area_factors, axis=1), ("lat", "lon"))
    zonal = lax.psum(partial_value, "lon")
    error_power_two, prediction_error, covariance_sum = stacked_metrics(
        zonal, horizon_tally, quantity_tally, float(lon_total)
    )
    total_square, total_offset, total_agree = stacked_metrics(
        grand[:, None], horizon_tally, quantity_tally, float(lat_total * lon_total)
    )
    rmse = jnp.sqrt(jnp.maximum(total_square[:, :, 0], minimum_divisor))
    return (
        error_power_two,
        prediction_error,
        covariance_sum,
        rmse,
        total_offset[:, :, 0],
        total_agree[:, :, 0],
    )


def solution(mesh):
    in_specs = (
        P(None, None, "lon", "lat"),
        P(None, "lon", "lat"),
        P(None, "lon", "lat"),
        P("lon", "lat"),
        P(),
    )
    out_specs = (P(None, None, "lat"), P(None, None, "lat"), P(None, None, "lat"), P(), P(), P())
    return jax.shard_map(local, mesh=mesh, in_specs=in_specs, out_specs=out_specs, check_vma=False)
```

profile of v0, /device:TPU:0, one launch (start us, length us, event | category | flops | bytes accessed | tf_op | source)
XLA Modules:
  0.0 119.7 jit_solution(12313264060658802673)
XLA Ops:
  7.2 0.0 copy-start.4
  7.2 0.6 sine_reduce_fusion
  7.8 1.3 %fusion.10 = (s32[]{:T(128)}, s32[]{:T(128)}) fusion(s32[4]{0:T(128)} %param.9, s32[]{:T(128)S(6)} %axis_index.15), kind=kLoop, calls=%fused_computation.33 | loop fusion | flops 22 | bytes 28 | tf_op jit(solution)/shard_map/reduce_sum | solution.py:48
  9.1 0.6 compare_convert_fusion
  9.8 0.0 copy-start
  9.8 0.0 copy-start.3
  9.8 1.9 %copy.18 = f32[69,45,128]{2,1,0:T(8,128)S(1)} copy(f32[69,45,128]{2,0,1:T(8,128)} %param.7) | data formatting | bytes 3179520 | tf_op args[2]
  11.8 0.5 copy-done.3
  12.2 0.3 fusion.3
  12.5 0.3 copy.19
  12.9 2.1 %copy-done.1 = f32[4,69,45,128]{3,0,2,1:T(4,128)S(1)} copy-done((f32[4,69,45,128]{3,0,2,1:T(4,128)S(1)}, f32[4,69,45,128]{3,0,2,1:T(4,128)}, u32[]{:S(2)}) %copy-start.1) | copy-done | bytes 6359064
  15.0 10.1 %fusion.1 = (f32[4,69,128]{2,0,1:T(4,128)S(1)}, f32[4,69,128]{2,0,1:T(4,128)S(1)}, f32[4,69,128]{2,0,1:T(4,128)S(1)}, f32[4,69,128]{2,0,1:T(4,128)S(1)}) fusion(f32[4,69,45,128]{3,0,2,1:T(4,128)S(1)} %copy-done.1, f32[69,45,128]{2,1,0:T(8,128)S(1)} %copy.19, f32[69,45,128]{2,1,0:T(8,128)S(1)} %copy.18, f32[45,128]{1,0:T(8,128)S(1)} %convert_multiply_fusion), kind=kLoop, calls=%fused_computation.5 | loop fusion | flops 17346048 | bytes 10126848 | tf_op jit(solution)/shard_map/reduce_sum | solution.py:70
  25.3 2.0 %compare_select_fusion.2 = f32[128]{0:T(128)S(1)} fusion(f32[]{:T(128)} %sine_reduce_fusion, s32[]{:T(128)} %get-tuple-element.22, s32[]{:T(128)} %get-tuple-element.23), kind=kLoop, calls=%fused_computation.30 | loop fusion | flops 896 | bytes 524 | tf_op jit(solution)/shard_map/jit(_where)/select_n | solution.py:55
  27.3 0.7 concatenate.3
  27.9 0.2 multiply_reduce_fusion.1
  28.2 0.0 all-reduce.2.cloned.1.call-start
  28.2 0.5 copy-done.2
  28.7 0.2 all-reduce.2.cloned.1.call-update
  28.9 42.2 %psum.15 = f32[1173]{0:T(1024)S(1)} all-reduce(f32[1173]{0:T(1024)S(1)} %multiply_reduce_fusion.1), channel_id=1, replica_groups=mesh['lat'=4,'lon'=8] {'lat','lon'}, use_global_device_ids=true, to_apply=%region_10.11 | all-reduce | flops 1173 | bytes 9384 | tf_op jit(solution)/shard_map/psum | solution.py:80
  71.1 0.1 fusion.6
  71.2 0.1 div.94
  71.3 0.1 max.48
  71.4 0.7 div.92
  72.0 0.7 sqrt.14
  72.7 0.1 fusion.11
  72.8 0.6 rsqrt_multiply_fusion.1
  73.4 35.3 %all-reduce.2.cloned.1.call-done = f32[1173,128]{1,0:T(8,128)} async-done(((f32[1173,128]{1,0:T(8,128)}), f32[1173,128]{1,0:T(8,128)}) %all-reduce.2.cloned.1.call-update) | async-done | bytes 600592 | tf_op jit(solution)/shard_map/psum | solution.py:81
  108.7 1.2 fusion.4
  109.9 0.8 fusion.5
  110.7 0.7 copy.26
  111.4 0.7 copy.24
  112.1 0.7 copy.25
  (18 shorter events, 0.2 us)
Async XLA Ops:
  7.2 4.6 %copy-start.4 = (s32[45,128]{1,0:T(8,128)S(1)}, s32[45,128]{1,0:T(8,128)}, u32[]{:S(2)}) copy-start(s32[45,128]{1,0:T(8,128)} %param.8) | copy-start | bytes 69124
  9.8 2.0 %copy-start = (f32[69,45,128]{2,0,1:T(8,128)S(1)}, f32[69,45,128]{2,0,1:T(8,128)}, u32[]{:S(2)}) copy-start(f32[69,45,128]{2,0,1:T(8,128)} %param.7) | copy-start | bytes 4769284
  9.8 2.4 %copy-start.3 = (f32[69,45,128]{2,0,1:T(8,128)S(1)}, f32[69,45,128]{2,0,1:T(8,128)}, u32[]{:S(2)}) copy-start(f32[69,45,128]{2,0,1:T(8,128)} %param.6) | copy-start | bytes 4769284
  12.2 2.8 %copy-start.1 = (f32[4,69,45,128]{3,0,2,1:T(4,128)S(1)}, f32[4,69,45,128]{3,0,2,1:T(4,128)}, u32[]{:S(2)}) copy-start(f32[4,69,45,128]{3,0,2,1:T(4,128)} %param.5) | copy-start | bytes 19077124
  27.9 0.8 copy-start.2
  28.2 80.5 %all-reduce.2.cloned.1.call-start = ((), (), s32[]{:S(2)}) async-start(), calls=%async_computation | async-start | bytes 1204224 | tf_op jit(solution)/shard_map/psum | solution.py:81
Sparse Core Ops, SparseCore 0:
  32.4 76.1 all-reduce.1
where the time goes:
time: 120 us
  blocking collectives  42.2 us (35%)
  waiting for transfers between devices  35.5 us (30%)
  other arithmetic  18 us (15%)
  between operations  14.2 us (12%)
  local copies, waits for them, and re-layouts  9.77 us (8%)
    psum x1, blocking collectives, local(): lax.psum(jnp.sum(partial_value * area_factors, axis=1), ('lat', 'lon'))  42.2 us
    psum x1, waiting for transfers between devices, local(): zonal = lax.psum(partial_value, 'lon')  35.3 us
    reduce_sum x1, other arithmetic, local(): jnp.sum(retained_entries * predicted_anomaly * observed_anomaly[None], ax...  10.1 us
    unnamed x14, local copies, waits for them, and re-layouts  7.14 us
  transfers between devices with their start and end apart: 1, of which 1 were waited for; matrix products, arithmetic and copies ran while one was open for 2% of the time, Pallas kernels for 0%

commit v1 on v0

--- a/solution.py
+++ b/solution.py
@@ -78,7 +78,7 @@
         axis=0,
     )
     grand = lax.psum(jnp.sum(partial_value * area_factors, axis=1), ("lat", "lon"))
-    zonal = lax.psum(partial_value, "lon")
+    zonal = jnp.sum(lax.all_gather(partial_value, "lon"), axis=0)
     error_power_two, prediction_error, covariance_sum = stacked_metrics(
         zonal, horizon_tally, quantity_tally, float(lon_total)
     )

time: 120 us -> 127 us (1.058)
  other arithmetic: 18 us -> 22.7 us
  blocking collectives: 42.2 us -> 43.9 us
    psum x1 -> x0, waiting for transfers between devices: 35.3 us -> none  [local(): zonal = lax.psum(partial_value, 'lon')]
    all_gather x0 -> x1, waiting for transfers between devices: none -> 34.8 us  [local(): zonal = jnp.sum(lax.all_gather(partial_value, 'lon'), axis=0)]
    concatenate x1, local copies, waits for them, and re-layouts: 0.66 us -> 4.81 us  [local(): jnp.concatenate([jnp.sum(retained_entries * mistake_field * mistake_field...]
    unnamed x14 -> x8, local copies, waits for them, and re-layouts: 7.14 us -> 4.02 us
    reduce_sum x0 -> x1, other arithmetic: none -> 2.66 us  [local(): zonal = jnp.sum(lax.all_gather(partial_value, 'lon'), axis=0)]
    reduce_sum x1, other arithmetic: 0.32 us -> 2.38 us  [local(): jnp.sum(retain_filter[None] * observed_anomaly * observed_anomaly, axis=1)]
    psum x1, blocking collectives: 42.2 us -> 43.9 us  [local(): lax.psum(jnp.sum(partial_value * area_factors, axis=1), ('lat', 'lon'))]
  transfers between devices with their start and end apart: 1 -> 1, of which waited for: 1 -> 1; matrix products, arithmetic and copies ran while one was open for 2% -> 5% of each run, Pallas kernels for 0% -> 0%
where the time goes in v1:
time: 127 us
  blocking collectives  43.9 us (35%)
  waiting for transfers between devices  34.9 us (27%)
  other arithmetic  22.7 us (18%)
  between operations  14.2 us (11%)
  local copies, waits for them, and re-layouts  10.8 us (9%)
    psum x1, blocking collectives, local(): lax.psum(jnp.sum(partial_value * area_factors, axis=1), ('lat', 'lon'))  43.9 us
    all_gather x1, waiting for transfers between devices, local(): zonal = jnp.sum(lax.all_gather(partial_value, 'lon'), axis=0)  34.8 us
    reduce_sum x1, other arithmetic, local(): jnp.sum(retained_entries * predicted_anomaly * observed_anomaly[None], ax...  10.2 us
    concatenate x1, local copies, waits for them, and re-layouts, local(): jnp.concatenate([jnp.sum(retained_entries * mistake_field * mistake_field...  4.81 us
    unnamed x8, local copies, waits for them, and re-layouts  4.02 us
    reduce_sum x1, other arithmetic, local(): zonal = jnp.sum(lax.all_gather(partial_value, 'lon'), axis=0)  2.66 us
  transfers between devices with their start and end apart: 1, of which 1 were waited for; matrix products, arithmetic and copies ran while one was open for 5% of the time, Pallas kernels for 0%

profile of v1, /device:TPU:0, one launch (start us, length us, event | category | flops | bytes accessed | tf_op | source)
XLA Modules:
  0.0 126.5 jit_solution(11009926272718569717)
XLA Ops:
  7.2 0.0 all-gather.4.cloned.1.call-start
  7.2 1.3 %fusion.10 = (s32[]{:T(128)}, s32[]{:T(128)}) fusion(s32[4]{0:T(128)} %param.9, s32[]{:T(128)S(6)} %axis_index.15), kind=kLoop, calls=%fused_computation.33 | loop fusion | flops 22 | bytes 28 | tf_op jit(solution)/shard_map/reduce_sum | solution.py:48
  8.5 0.6 compare_convert_fusion
  9.2 0.0 slice-start
  9.2 1.9 %copy.18 = f32[69,45,128]{2,1,0:T(8,128)S(1)} copy(f32[69,45,128]{2,0,1:T(8,128)} %param.7) | data formatting | bytes 3179520 | tf_op args[2]
  11.1 0.7 convert_multiply_fusion
  11.9 0.0 slice-start.1
  11.9 2.4 %fusion.3 = (f32[69,128]{1,0:T(8,128)S(1)}, f32[69,45,128]{2,0,1:T(8,128)S(1)}) fusion(f32[45,128]{1,0:T(8,128)S(1)} %convert_multiply_fusion, f32[69,45,128]{2,0,1:T(8,128)} %param.6, f32[69,45,128]{2,0,1:T(8,128)} %param.7), kind=kLoop, calls=%fused_computation.8 | loop fusion | flops 1580928 | bytes 4827648 | tf_op jit(solution)/shard_map/reduce_sum | solution.py:76
  14.2 0.3 copy.19
  14.6 0.0 slice-done
  14.6 0.0 slice-done.1
  14.6 10.2 %fusion.1 = (f32[4,69,128]{2,0,1:T(4,128)S(1)}, f32[4,69,128]{2,0,1:T(4,128)S(1)}, f32[4,69,128]{2,0,1:T(4,128)S(1)}, f32[4,69,128]{2,0,1:T(4,128)S(1)}) fusion(f32[4,69,45,128]{3,0,2,1:T(4,128)S(1)} %bitcast.2, f32[69,45,128]{2,1,0:T(8,128)S(1)} %copy.19, f32[69,45,128]{2,1,0:T(8,128)S(1)} %copy.18, f32[45,128]{1,0:T(8,128)S(1)} %convert_multiply_fusion), kind=kLoop, calls=%fused_computation.5 | loop fusion | flops 17346048 | bytes 10126848 | tf_op jit(solution)/shard_map/reduce_sum | solution.py:70
  24.9 4.8 %concatenate.3 = f32[1173,128]{1,0:T(8,128)} concatenate(f32[276,128]{1,0:T(8,128)S(1)} %reshape.153, f32[276,128]{1,0:T(8,128)S(1)} %reshape.154, f32[276,128]{1,0:T(8,128)S(1)} %reshape.155, f32[276,128]{1,0:T(8,128)S(1)} %reshape.156, f32[69,128]{1,0:T(8,128)S(1)} %get-tuple-element.24), dimensions={0} | concatenate | bytes 1201152 | tf_op jit(solution)/shard_map/concatenate | solution.py:64
  29.8 0.0 all-gather.4.cloned.1.call-update
  29.8 0.6 sine_reduce_fusion
  30.4 2.0 %compare_select_fusion.2 = f32[128]{0:T(128)S(1)} fusion(f32[]{:T(128)} %sine_reduce_fusion, s32[]{:T(128)} %get-tuple-element.22, s32[]{:T(128)} %get-tuple-element.23), kind=kLoop, calls=%fused_computation.30 | loop fusion | flops 896 | bytes 524 | tf_op jit(solution)/shard_map/jit(_where)/select_n | solution.py:55
  32.4 1.3 %multiply_reduce_fusion.1 = f32[1173]{0:T(1024)S(1)} fusion(f32[1173,128]{1,0:T(8,128)} %concatenate.3, f32[128]{0:T(128)S(1)} %compare_select_fusion.2), kind=kLoop, calls=%fused_computation.9 | loop fusion | flops 299115 | bytes 605780 | tf_op jit(solution)/shard_map/reduce_sum | solution.py:80
  33.7 43.9 %psum.7 = f32[1173]{0:T(1024)S(1)} all-reduce(f32[1173]{0:T(1024)S(1)} %multiply_reduce_fusion.1), channel_id=1, replica_groups=mesh['lat'=4,'lon'=8] {'lat','lon'}, use_global_device_ids=true, to_apply=%region_10.11 | all-reduce | flops 1173 | bytes 9384 | tf_op jit(solution)/shard_map/psum | solution.py:80
  77.6 0.1 fusion.6
  77.7 0.1 div.94
  77.8 0.1 max.48
  77.9 0.7 div.92
  78.5 0.7 sqrt.14
  79.2 0.1 fusion.11
  79.3 0.6 rsqrt_multiply_fusion.1
  79.9 34.8 %all-gather.4.cloned.1.call-done = f32[8,1173,128]{2,1,0:T(8,128)} async-done(((f32[1,1173,128]{2,1,0:T(8,128)}), f32[8,1173,128]{2,1,0:T(8,128)}) %all-gather.4.cloned.1.call-update) | async-done | bytes 4804624 | tf_op jit(solution)/shard_map/all_gather | solution.py:81
  114.7 2.7 %reduce_sum.96 = f32[1173,128]{1,0:T(8,128)S(1)} reduce(f32[8,1173,128]{2,1,0:T(8,128)} %all-gather.4.cloned.1.call-done, f32[]{:T(128)} %constant.36.clone.1), dimensions={0}, to_apply=%region_6.7 | reduce | flops 1051008 | bytes 5405188 | tf_op jit(solution)/shard_map/reduce_sum | solution.py:81
  117.4 0.1 fusion.4
  117.5 0.7 copy.26
  118.2 0.7 copy.24
  119.0 0.7 copy.25
  (15 shorter events, 0.2 us)
Async XLA Ops:
  7.2 107.5 %all-gather.4.cloned.1.call-start = ((), (), s32[]{:S(2)}) async-start(), calls=%async_computation | async-start | bytes 5419008 | tf_op jit(solution)/shard_map/all_gather | solution.py:81
  9.2 5.4 %slice-start = ((s8[6359040]{0:T(1024)(128)(4,1)}), s8[4194304]{0:T(1024)(128)(4,1)S(1)}, s32[]{:S(2)}) async-start(s8[6359040]{0:T(1024)(128)(4,1)} %bitcast.1), calls=%async_computation.1 | async-start | bytes 8388608
  11.9 2.7 %slice-start.1 = ((s8[6359040]{0:T(1024)(128)(4,1)}), s8[2164736]{0:T(1024)(128)(4,1)S(1)}, s32[]{:S(2)}) async-start(s8[6359040]{0:T(1024)(128)(4,1)} %bitcast.1), calls=%async_computation.2 | async-start | bytes 4329472
Sparse Core Ops, SparseCore 0:
  29.9 84.7 all-gather.3
